TPU v7x, 32 devices: a whole 2x2x4 slice. The times are simulated.
32 devices in a mesh: grp: 2 (over y), kvp: 4 (over x, core), tp: 4 (over z).
Axes of the slice: x: 2, y: 2, z: 4, core: 2. Of those that a mesh axis runs over, the one named last changes fastest.
Arguments:
- hidden_in: bfloat16 [16, 7168], P('grp'), parts along dimension 0, may hold values from -3 to 3
- queries_nope: bfloat16 [16, 128, 128], P('grp', ('kvp', 'tp')), parts along dimension 0, may hold values from -6 to 6
- queries_rope: bfloat16 [16, 128, 64], P('grp', ('kvp', 'tp')), parts along dimension 0, may hold values from -26 to 26
- cache: bfloat16 [16, 1536, 576], P('grp', 'kvp'), parts along dimension 0, may hold values from -20 to 20
- lengths: int32 [16], P('grp'), parts along dimension 0, may hold values from 128 to 1536, as said below
- w_uk: bfloat16 [128, 128, 512], P(('kvp', 'tp')), may hold values from -0.5 to 0.5
- w_uv: bfloat16 [128, 512, 128], P(('kvp', 'tp')), may hold values from -0.25 to 0.25
- w_out: bfloat16 [16384, 7168], P(('kvp', 'tp')), may hold values from -0.0625 to 0.0625
- norm_gain: float32 [7168], replicated, may hold values from 0.25 to 1.75
- w_gate: bfloat16 [7168, 18432], P(None, ('kvp', 'tp')), may hold values from -0.0625 to 0.0625
- w_up: bfloat16 [7168, 18432], P(None, ('kvp', 'tp')), may hold values from -0.0625 to 0.0625
- w_down: bfloat16 [18432, 7168], P(('kvp', 'tp')), may hold values from -0.0625 to 0.0625
Outputs:
- layer_out: bfloat16 [16, 7168], P('grp', ('kvp', 'tp')), parts along dimension 0
There are 2 independent parts, one for each index of `grp`. A program takes and returns all parts, laid end to end along the dimension named above; an argument that names none is the same for every part. Nothing has to cross between parts.
Inputs may be any that keep to these rules, and one draw needn't show every extreme that they name: `lengths`: every length is a multiple of 128; in every draw some request has the full 1536.
All inputs are finite; a program needn't handle non-finite values.
Results may differ from a plain program's by a relative error of at most 0.04.
Values may be sent and summed in bfloat16 or wider, within the bound.
A program may use at most 128 MiB of HBM per device.

v0:
```python
import jax
import jax.numpy as jnp
from jax import lax
from jax.sharding import PartitionSpec as P


def project(o_lat, w_uv, w_out):
    head_out = jnp.einsum("bhl,hle->bhe", o_lat, w_uv, preferred_element_type=jnp.float32).astype(
        jnp.bfloat16
    )
    return jnp.dot(
        head_out.reshape(head_out.shape[0], -1), w_out, preferred_element_type=jnp.float32
    )


def per_device(
    hidden_in,
    queries_nope,
    queries_rope,
    cache,
    lengths,
    w_uk,
    w_uv,
    w_out,
    norm_gain,
    w_gate,
    w_up,
    w_down,
):
    batch, heads_dev, head_dim = queries_nope.shape
    latent = w_uk.shape[2]
    ctx_dev = cache.shape[1]
    groups = lax.axis_size("kvp")
    score_scale = float(head_dim + queries_rope.shape[2]) ** (-0.5)
    q_lat = jnp.einsum(
        "bhd,hdl->bhl", queries_nope, w_uk, preferred_element_type=jnp.float32
    ).astype(jnp.bfloat16)
    q_lat_all, rope_all = (
        lax.all_gather(q_lat, "kvp", axis=1, tiled=True),
        lax.all_gather(queries_rope, "kvp", axis=1, tiled=True),
    )
    q_full = jnp.concatenate([q_lat_all, rope_all], axis=2)
    scores = (
        jnp.einsum("bhc,btc->bht", q_full, cache, preferred_element_type=jnp.float32) * score_scale
    )
    offset = lax.axis_index("kvp") * ctx_dev
    visible = ((offset + jnp.arange(ctx_dev, dtype=jnp.int32))[None, :] < lengths[:, None])[
        :, None, :
    ]
    masked = jnp.where(visible, scores, jnp.float32(-1e30))
    block_max = jnp.max(masked, axis=2)
    exponent = jnp.where(visible, jnp.exp(masked - block_max[..., None]), jnp.float32(0.0))
    guarded = jnp.maximum(jnp.sum(exponent, axis=2), 1.0)
    log_total = block_max + jnp.log(guarded)
    weights = (exponent / guarded[..., None]).astype(jnp.bfloat16)
    partial_value = jnp.einsum("bht,btc->bhc", weights, cache, preferred_element_type=jnp.float32)[
        ..., :latent
    ]
    blocks = partial_value.reshape(batch, groups, heads_dev, latent)
    block_logs = log_total.reshape(batch, groups, heads_dev)
    part_blocks = lax.all_to_all(
        blocks.astype(jnp.bfloat16), "kvp", split_axis=1, concat_axis=1, tiled=True
    ).astype(blocks.dtype)
    part_logs = lax.all_to_all(
        block_logs.astype(jnp.bfloat16), "kvp", split_axis=1, concat_axis=1, tiled=True
    ).astype(block_logs.dtype)
    highest = jnp.max(part_logs, axis=1)
    overall = highest + jnp.log(jnp.sum(jnp.exp(part_logs - highest[:, None, :]), axis=1))
    scaled = jnp.exp(part_logs - overall[:, None, :])[..., None] * part_blocks
    o_lat = jnp.sum(scaled, axis=1).astype(jnp.bfloat16)
    attention = project(o_lat, w_uv, w_out)
    model_width = norm_gain.shape[0]
    share_width = model_width // lax.axis_size(("kvp", "tp"))
    share_start = lax.axis_index(("kvp", "tp")) * share_width
    attn_whole = lax.psum(attention, ("kvp", "tp"))
    residual = hidden_in.astype(jnp.float32) + attn_whole
    mean_square = jnp.mean(residual * residual, axis=1)
    normed = (residual * lax.rsqrt(mean_square + 1e-06)[:, None] * norm_gain[None, :]).astype(
        jnp.bfloat16
    )
    residual_share = lax.dynamic_slice_in_dim(residual, share_start, share_width, 1)
    gate_proj = jnp.dot(normed, w_gate, preferred_element_type=jnp.float32)
    up_proj = jnp.dot(normed, w_up, preferred_element_type=jnp.float32)
    act = (jax.nn.silu(gate_proj) * up_proj).astype(jnp.bfloat16)
    ffn_terms = jnp.dot(act, w_down, preferred_element_type=jnp.float32)
    ffn_share = lax.psum_scatter(ffn_terms, ("kvp", "tp"), scatter_dimension=1, tiled=True)
    return (residual_share + ffn_share).astype(jnp.bfloat16)


def solution(mesh):
    placed = (
        P("grp", None),
        P("grp", ("kvp", "tp"), None),
        P("grp", ("kvp", "tp"), None),
        P("grp", "kvp", None),
        P("grp"),
        P(("kvp", "tp"), None, None),
        P(("kvp", "tp"), None, None),
        P(("kvp", "tp"), None),
        P(),
        P(None, ("kvp", "tp")),
        P(None, ("kvp", "tp")),
        P(("kvp", "tp"), None),
    )
    return jax.shard_map(
        per_device, mesh=mesh, in_specs=placed, out_specs=P("grp", ("kvp", "tp")), check_vma=False
    )
```

profile of v0, /device:TPU:0, one launch (start us, length us, event | category | flops | bytes accessed | tf_op | source)
XLA Modules:
  0.0 248.7 jit_solution(1045707272200250479)
XLA Ops:
  6.5 0.0 copy-start
  6.5 0.9 copy.24
  7.4 6.3 %all_gather.7 = bf16[8,32,64]{2,0,1:T(8,128)(2,1)S(1)} all-gather(bf16[8,8,64]{2,0,1:T(8,128)(2,1)S(1)} %copy.24), channel_id=1, replica_groups=mesh['grp'=2,'kvp'=4,'tp'=4] {'kvp'}, dimensions={1}, use_global_device_ids=true | all-gather | bytes 40960 | tf_op jit(solution)/shard_map/all_gather | solution.py:40
  13.7 1.5 fusion.2
  15.2 6.3 %all_gather.6 = bf16[8,32,512]{2,0,1:T(8,128)(2,1)S(1)} all-gather(bf16[8,8,512]{2,0,1:T(8,128)(2,1)S(1)} %fusion.2), channel_id=1, replica_groups=mesh['grp'=2,'kvp'=4,'tp'=4] {'kvp'}, dimensions={1}, use_global_device_ids=true | all-gather | bytes 327680 | tf_op jit(solution)/shard_map/all_gather | solution.py:39
  21.5 0.1 copy.25
  21.6 0.7 broadcast_compare_fusion
  22.3 0.0 copy-done
  22.3 0.7 fusion.31
  23.0 0.0 copy-start.3
  23.0 0.7 copy-done.3
  23.8 0.2 fusion.8
  24.0 0.6 add_convert_fusion.1
  24.6 0.8 convert_element_type.50
  25.3 0.6 copy.27
  25.9 3.2 %all-to-all-start = ((bf16[8,4,8]{2,0,1:T(8,128)(2,1)}), bf16[8,4,8]{2,0,1:T(8,128)(2,1)S(1)}, u32[]{:S(2)}, u32[]{:S(2)}) async-start(bf16[8,4,8]{2,0,1:T(8,128)(2,1)} %copy.27), calls=%async_computation | async-start | bytes 16384 | tf_op jit(solution)/shard_map/all_to_all | solution.py:64
  29.2 2.2 fusion.10
  31.4 0.0 copy-start.5
  31.5 0.0 copy-start.4
  31.5 0.7 copy.28
  32.2 0.8 all-to-all-done
  33.0 3.4 %all-to-all-start.1 = ((bf16[8,4,8,512]{3,2,0,1:T(8,128)(2,1)}), bf16[8,4,8,512]{3,2,0,1:T(8,128)(2,1)S(1)}, u32[]{:S(2)}, u32[]{:S(2)}) async-start(bf16[8,4,8,512]{3,2,0,1:T(8,128)(2,1)} %copy.28), calls=%async_computation.1 | async-start | bytes 524288 | tf_op jit(solution)/shard_map/all_to_all | solution.py:61
  36.4 0.0 all-reduce.2.cloned.1.call-start
  36.5 5.8 %all-to-all-done.1 = bf16[8,4,8,512]{3,2,0,1:T(8,128)(2,1)S(1)} async-done(((bf16[8,4,8,512]{3,2,0,1:T(8,128)(2,1)}), bf16[8,4,8,512]{3,2,0,1:T(8,128)(2,1)S(1)}, u32[]{:S(2)}, u32[]{:S(2)}) %all-to-all-start.1) | async-done | bytes 262176 | tf_op jit(solution)/shard_map/all_to_all | solution.py:61
  42.4 0.1 multiply_reduce_fusion
  42.5 8.4 %fusion.4 = f32[8,7168]{1,0:T(8,128)} fusion(bf16[1024,7168]{1,0:T(8,128)(2,1)} %param.19, bf16[8,512,128]{2,1,0:T(8,128)(2,1)} %param.18, bf16[8,8,512]{2,1,0:T(8,128)(2,1)S(1)} %multiply_reduce_fusion), kind=kOutput, calls=%fused_computation.9 | convolution fusion | flops 125837312 | bytes 16023552 | tf_op jit(solution)/shard_map/dot_general | solution.py:11
  50.8 0.0 all-reduce.2.cloned.1.call-update
  50.9 0.0 reduce-scatter.4.cloned.1.call-start
  50.9 89.8 %all-reduce.2.cloned.1.call-done = f32[8,7168]{1,0:T(8,128)} async-done(((f32[8,7168]{1,0:T(8,128)}), f32[8,7168]{1,0:T(8,128)}) %all-reduce.2.cloned.1.call-update) | async-done | bytes 229392 | tf_op jit(solution)/shard_map/psum | solution.py:75
  140.7 0.0 copy-done.5
  140.7 1.1 multiply_reduce_fusion.1
  141.8 0.0 copy-start.2
  141.8 0.7 copy-done.2
  142.5 0.0 copy-done.4
  142.5 8.6 %fusion.30 = f32[8,1152]{1,0:T(8,128)} fusion(bf16[7168,1152]{1,0:T(8,128)(2,1)} %param.21, f32[8,7168]{1,0:T(8,128)S(1)} %get-tuple-element.6, f32[7168]{0:T(1024)S(1)} %copy-done.4, f32[8]{0:T(128)S(1)} %add_rsqrt_fusion), kind=kOutput, calls=%fused_computation.50 | convolution fusion | flops 132292608 | bytes 16810016 | tf_op jit(solution)/shard_map/dot_general | solution.py:82
  151.1 0.0 copy-start.1
  151.1 18.6 %convolution_bitcast_fusion = f32[7168,8]{1,0:T(8,128)} fusion(bf16[1152,7168]{1,0:T(8,128)(2,1)} %param.23, bf16[7168,1152]{1,0:T(8,128)(2,1)} %param.22, f32[8,1152]{1,0:T(8,128)} %fusion.30, f32[8,7168]{1,0:T(8,128)} %copy-done.2, f32[7168]{0:T(1024)} %param.20, f32[8]{0:T(128)S(1)} %add_rsqrt_fusion), kind=kOutput, calls=%fused_computation | convolution fusion | flops 264468480 | bytes 33554464
  169.7 0.0 reduce-scatter.4.cloned.1.call-update
  169.7 69.7 %reduce-scatter.4.cloned.1.call-done = f32[448,8]{1,0:T(8,128)} async-done(((f32[7168,8]{1,0:T(8,128)}), f32[448,8]{1,0:T(8,128)}) %reduce-scatter.4.cloned.1.call-update) | async-done | bytes 14352
  239.4 1.0 copy.32
  240.4 1.4 add_convert_fusion
  241.9 0.0 copy-done.1
  (9 shorter events, 0.1 us)
Async XLA Ops:
  6.5 15.7 %copy-start = (bf16[8,384,576]{1,2,0:T(8,128)(2,1)S(1)}, bf16[8,384,576]{1,2,0:T(8,128)(2,1)}, u32[]{:S(2)}) copy-start(bf16[8,384,576]{1,2,0:T(8,128)(2,1)} %param.15) | copy-start | bytes 10616836
  23.0 0.7 copy-start.3
  25.9 7.0 %all-to-all-start = ((bf16[8,4,8]{2,0,1:T(8,128)(2,1)}), bf16[8,4,8]{2,0,1:T(8,128)(2,1)S(1)}, u32[]{:S(2)}, u32[]{:S(2)}) async-start(bf16[8,4,8]{2,0,1:T(8,128)(2,1)} %copy.27), calls=%async_computation | async-start | bytes 16384 | tf_op jit(solution)/shard_map/all_to_all | solution.py:64
  31.4 109.2 %copy-start.5 = (bf16[8,7168]{1,0:T(8,128)(2,1)S(1)}, bf16[8,7168]{1,0:T(8,128)(2,1)}, u32[]{:S(2)}) copy-start(bf16[8,7168]{1,0:T(8,128)(2,1)} %param.12) | copy-start | bytes 344068
  31.5 111.0 %copy-start.4 = (f32[7168]{0:T(1024)S(1)}, f32[7168]{0:T(1024)}, u32[]{:S(2)}) copy-start(f32[7168]{0:T(1024)} %param.20) | copy-start | bytes 86020
  33.0 9.4 %all-to-all-start.1 = ((bf16[8,4,8,512]{3,2,0,1:T(8,128)(2,1)}), bf16[8,4,8,512]{3,2,0,1:T(8,128)(2,1)S(1)}, u32[]{:S(2)}, u32[]{:S(2)}) async-start(bf16[8,4,8,512]{3,2,0,1:T(8,128)(2,1)} %copy.28), calls=%async_computation.1 | async-start | bytes 524288 | tf_op jit(solution)/shard_map/all_to_all | solution.py:61
  36.4 104.3 %all-reduce.2.cloned.1.call-start = ((), (), s32[]{:S(2)}) async-start(), calls=%async_computation.3 | async-start | bytes 458752 | tf_op jit(solution)/shard_map/psum | solution.py:75
  50.9 188.6 %reduce-scatter.4.cloned.1.call-start = ((), (), s32[]{:S(2)}) async-start(), calls=%async_computation.4 | async-start | bytes 3899392
  141.8 0.7 copy-start.2
  151.1 90.8 %copy-start.1 = (bf16[8,384,576]{1,2,0:T(8,128)(2,1)S(1)}, bf16[8,384,576]{1,2,0:T(8,128)(2,1)}, u32[]{:S(2)}) copy-start(bf16[8,384,576]{1,2,0:T(8,128)(2,1)} %param.15) | copy-start | bytes 10616836
Sparse Core Ops, SparseCore 0:
  51.0 89.6 all-reduce.1
  169.9 69.5 reduce-scatter.3
where the time goes:
time: 249 us
  waiting for transfers between devices  166 us (67%)
  matrix products  40 us (16%)
  between operations  13.5 us (5%)
  blocking collectives  12.6 us (5%)
  starting transfers between devices  6.74 us (3%)
  local copies, waits for them, and re-layouts  5.54 us (2%)
  other arithmetic  4.23 us (2%)
    psum x1, waiting for transfers between devices, per_device(): attn_whole = lax.psum(attention, ('kvp', 'tp'))  89.8 us
    unnamed x3, waiting for transfers between devices  69.7 us
    unnamed x1, matrix products  18.6 us
    dot_general x1, matrix products, per_device(): gate_proj = jnp.dot(normed, w_gate, preferred_element_type=jnp.float32)  8.58 us
    dot_general x1, matrix products, project(): jnp.dot(head_out.reshape(head_out.shape[0], -1), w_out, preferred_element...  8.36 us
    all_gather x1, blocking collectives, per_device(): lax.all_gather(queries_rope, 'kvp', axis=1, tiled=True)  6.3 us
    all_gather x1, blocking collectives, per_device(): lax.all_gather(q_lat, 'kvp', axis=1, tiled=True)  6.27 us
    all_to_all x1, waiting for transfers between devices, per_device(): lax.all_to_all(blocks.astype(jnp.bfloat16), 'kvp', split_axis=1, concat_a...  5.84 us
  transfers between devices with their start and end apart: 4, of which 4 were waited for; matrix products, arithmetic and copies ran while one was open for 1% of the time, Pallas kernels for 0%

commit v1 on v0

--- a/solution.py
+++ b/solution.py
@@ -72,7 +72,7 @@
     model_width = norm_gain.shape[0]
     share_width = model_width // lax.axis_size(("kvp", "tp"))
     share_start = lax.axis_index(("kvp", "tp")) * share_width
-    attn_whole = lax.psum(attention, ("kvp", "tp"))
+    attn_whole = jnp.sum(lax.all_gather(attention, ("kvp", "tp")), axis=0)
     residual = hidden_in.astype(jnp.float32) + attn_whole
     mean_square = jnp.mean(residual * residual, axis=1)
     normed = (residual * lax.rsqrt(mean_square + 1e-06)[:, None] * norm_gain[None, :]).astype(

time: 249 us -> 207 us (0.83)
  waiting for transfers between devices: 166 us -> 122 us
    psum x1 -> x0, waiting for transfers between devices: 89.8 us -> none  [per_device(): attn_whole = lax.psum(attention, ('kvp', 'tp'))]
    all_gather x0 -> x1, waiting for transfers between devices: none -> 48.2 us  [per_device(): attn_whole = jnp.sum(lax.all_gather(attention, ('kvp', 'tp')), axis=0)]
where the time goes in v1:
time: 207 us; the launch traced here: 206 us
  waiting for transfers between devices  122 us (59%)
  matrix products  40 us (19%)
  between operations  13.5 us (7%)
  blocking collectives  12.6 us (6%)
  starting transfers between devices  6.74 us (3%)
  local copies, waits for them, and re-layouts  5.54 us (3%)
  other arithmetic  5.52 us (3%)
    unnamed x3, waiting for transfers between devices  67.6 us
    all_gather x1, waiting for transfers between devices, per_device(): attn_whole = jnp.sum(lax.all_gather(attention, ('kvp', 'tp')), axis=0)  48.2 us
    unnamed x1, matrix products  18.6 us
    dot_general x1, matrix products, per_device(): gate_proj = jnp.dot(normed, w_gate, preferred_element_type=jnp.float32)  8.58 us
    dot_general x1, matrix products, project(): jnp.dot(head_out.reshape(head_out.shape[0], -1), w_out, preferred_element...  8.35 us
    all_gather x1, blocking collectives, per_device(): lax.all_gather(queries_rope, 'kvp', axis=1, tiled=True)  6.3 us
    all_gather x1, blocking collectives, per_device(): lax.all_gather(q_lat, 'kvp', axis=1, tiled=True)  6.27 us
    all_to_all x1, waiting for transfers between devices, per_device(): lax.all_to_all(blocks.astype(jnp.bfloat16), 'kvp', split_axis=1, concat_a...  5.84 us
  transfers between devices with their start and end apart: 4, of which 4 were waited for; matrix products, arithmetic and copies ran while one was open for 1% of the time, Pallas kernels for 0%

profile of v1, /device:TPU:0, one launch (start us, length us, event | category | flops | bytes accessed | tf_op | source)
XLA Modules:
  0.0 206.3 jit_solution(16578285809508608998)
XLA Ops:
  6.5 0.0 copy-start
  6.5 0.9 copy.24
  7.4 6.3 %all_gather.13 = bf16[8,32,64]{2,0,1:T(8,128)(2,1)S(1)} all-gather(bf16[8,8,64]{2,0,1:T(8,128)(2,1)S(1)} %copy.24), channel_id=1, replica_groups=mesh['grp'=2,'kvp'=4,'tp'=4] {'kvp'}, dimensions={1}, use_global_device_ids=true | all-gather | bytes 40960 | tf_op jit(solution)/shard_map/all_gather | solution.py:40
  13.7 1.5 fusion.2
  15.2 6.3 %all_gather.12 = bf16[8,32,512]{2,0,1:T(8,128)(2,1)S(1)} all-gather(bf16[8,8,512]{2,0,1:T(8,128)(2,1)S(1)} %fusion.2), channel_id=1, replica_groups=mesh['grp'=2,'kvp'=4,'tp'=4] {'kvp'}, dimensions={1}, use_global_device_ids=true | all-gather | bytes 327680 | tf_op jit(solution)/shard_map/all_gather | solution.py:39
  21.5 0.1 copy.25
  21.6 0.7 broadcast_compare_fusion
  22.3 0.0 copy-done
  22.3 0.7 fusion.31
  23.0 0.0 copy-start.3
  23.0 0.7 copy-done.3
  23.8 0.2 fusion.8
  24.0 0.6 add_convert_fusion.1
  24.6 0.8 convert_element_type.50
  25.3 0.6 copy.27
  25.9 3.2 %all-to-all-start = ((bf16[8,4,8]{2,0,1:T(8,128)(2,1)}), bf16[8,4,8]{2,0,1:T(8,128)(2,1)S(1)}, u32[]{:S(2)}, u32[]{:S(2)}) async-start(bf16[8,4,8]{2,0,1:T(8,128)(2,1)} %copy.27), calls=%async_computation | async-start | bytes 16384 | tf_op jit(solution)/shard_map/all_to_all | solution.py:64
  29.2 2.2 %fusion.10 = bf16[8,32,576]{2,1,0:T(8,128)(2,1)S(1)} fusion(bf16[8,384,576]{1,2,0:T(8,128)(2,1)S(1)} %copy-done, f32[8,32,384]{2,1,0:T(8,128)} %copy-done.3, f32[8,32]{1,0:T(8,128)} %get-tuple-element.8, f32[8,32]{1,0:T(8,128)S(1)} %get-tuple-element.9, pred[8,384]{1,0:T(8,128)(4,1)S(1)} %broadcast_compare_fusion), kind=kOutput, calls=%fused_computation.23 | convolution fusion | flops 113639424 | bytes 4232192 | tf_op jit(solution)/shard_map/bht,btc->bhc/dot_general | solution.py:56
  31.4 0.0 copy-start.5
  31.5 0.0 copy-start.4
  31.5 0.7 copy.28
  32.2 0.8 all-to-all-done
  33.0 3.4 %all-to-all-start.1 = ((bf16[8,4,8,512]{3,2,0,1:T(8,128)(2,1)}), bf16[8,4,8,512]{3,2,0,1:T(8,128)(2,1)S(1)}, u32[]{:S(2)}, u32[]{:S(2)}) async-start(bf16[8,4,8,512]{3,2,0,1:T(8,128)(2,1)} %copy.28), calls=%async_computation.1 | async-start | bytes 524288 | tf_op jit(solution)/shard_map/all_to_all | solution.py:61
  36.4 0.0 all-gather.3.cloned.1.call-start
  36.5 5.8 %all-to-all-done.1 = bf16[8,4,8,512]{3,2,0,1:T(8,128)(2,1)S(1)} async-done(((bf16[8,4,8,512]{3,2,0,1:T(8,128)(2,1)}), bf16[8,4,8,512]{3,2,0,1:T(8,128)(2,1)S(1)}, u32[]{:S(2)}, u32[]{:S(2)}) %all-to-all-start.1) | async-done | bytes 262176 | tf_op jit(solution)/shard_map/all_to_all | solution.py:61
  42.4 0.1 multiply_reduce_fusion
  42.5 8.3 %fusion.4 = f32[8,7168]{1,0:T(8,128)} fusion(bf16[1024,7168]{1,0:T(8,128)(2,1)} %param.19, bf16[8,512,128]{2,1,0:T(8,128)(2,1)} %param.18, bf16[8,8,512]{2,1,0:T(8,128)(2,1)S(1)} %multiply_reduce_fusion), kind=kOutput, calls=%fused_computation.10 | convolution fusion | flops 125837312 | bytes 16023552 | tf_op jit(solution)/shard_map/dot_general | solution.py:11
  50.8 0.0 all-gather.3.cloned.1.call-update
  50.9 0.0 reduce-scatter.4.cloned.1.call-start
  50.9 48.2 %all-gather.3.cloned.1.call-done = f32[128,7168]{1,0:T(8,128)} async-done(((f32[8,7168]{1,0:T(8,128)}), f32[128,7168]{1,0:T(8,128)}) %all-gather.3.cloned.1.call-update) | async-done | bytes 3670032 | tf_op jit(solution)/shard_map/all_gather | solution.py:75
  99.1 2.2 %bitcast_reduce_fusion = f32[8,7168]{1,0:T(8,128)S(1)} fusion(f32[128,7168]{1,0:T(8,128)} %all-gather.3.cloned.1.call-done), kind=kLoop, calls=%fused_computation.1 | loop fusion | flops 860160 | bytes 3899392 | tf_op jit(solution)/shard_map/reduce_sum | solution.py:75
  101.3 0.0 copy-done.5
  101.3 0.2 multiply_reduce_fusion.1
  101.5 0.0 copy-start.2
  101.5 0.7 copy-done.2
  102.2 0.0 copy-done.4
  102.2 8.6 %fusion.30 = f32[8,1152]{1,0:T(8,128)} fusion(bf16[7168,1152]{1,0:T(8,128)(2,1)} %param.21, f32[8,7168]{1,0:T(8,128)S(1)} %get-tuple-element.6, f32[7168]{0:T(1024)S(1)} %copy-done.4, f32[8]{0:T(128)S(1)} %add_rsqrt_fusion), kind=kOutput, calls=%fused_computation.51 | convolution fusion | flops 132292608 | bytes 16810016 | tf_op jit(solution)/shard_map/dot_general | solution.py:82
  110.8 0.0 copy-start.1
  110.8 18.6 %convolution_bitcast_fusion = f32[7168,8]{1,0:T(8,128)} fusion(bf16[1152,7168]{1,0:T(8,128)(2,1)} %param.23, bf16[7168,1152]{1,0:T(8,128)(2,1)} %param.22, f32[8,1152]{1,0:T(8,128)} %fusion.30, f32[8,7168]{1,0:T(8,128)} %copy-done.2, f32[7168]{0:T(1024)} %param.20, f32[8]{0:T(128)S(1)} %add_rsqrt_fusion), kind=kOutput, calls=%fused_computation | convolution fusion | flops 264468480 | bytes 33554464
  129.4 0.0 reduce-scatter.4.cloned.1.call-update
  129.5 67.6 %reduce-scatter.4.cloned.1.call-done = f32[448,8]{1,0:T(8,128)} async-done(((f32[7168,8]{1,0:T(8,128)}), f32[448,8]{1,0:T(8,128)}) %reduce-scatter.4.cloned.1.call-update) | async-done | bytes 14352
  197.0 1.0 copy.32
  198.0 1.4 add_convert_fusion
  199.5 0.0 copy-done.1
  (9 shorter events, 0.1 us)
Async XLA Ops:
  6.5 15.7 %copy-start = (bf16[8,384,576]{1,2,0:T(8,128)(2,1)S(1)}, bf16[8,384,576]{1,2,0:T(8,128)(2,1)}, u32[]{:S(2)}) copy-start(bf16[8,384,576]{1,2,0:T(8,128)(2,1)} %param.15) | copy-start | bytes 10616836
  23.0 0.7 copy-start.3
  25.9 7.0 %all-to-all-start = ((bf16[8,4,8]{2,0,1:T(8,128)(2,1)}), bf16[8,4,8]{2,0,1:T(8,128)(2,1)S(1)}, u32[]{:S(2)}, u32[]{:S(2)}) async-start(bf16[8,4,8]{2,0,1:T(8,128)(2,1)} %copy.27), calls=%async_computation | async-start | bytes 16384 | tf_op jit(solution)/shard_map/all_to_all | solution.py:64
  31.4 69.9 %copy-start.5 = (bf16[8,7168]{1,0:T(8,128)(2,1)S(1)}, bf16[8,7168]{1,0:T(8,128)(2,1)}, u32[]{:S(2)}) copy-start(bf16[8,7168]{1,0:T(8,128)(2,1)} %param.12) | copy-start | bytes 344068
  31.5 70.8 %copy-start.4 = (f32[7168]{0:T(1024)S(1)}, f32[7168]{0:T(1024)}, u32[]{:S(2)}) copy-start(f32[7168]{0:T(1024)} %param.20) | copy-start | bytes 86020
  33.0 9.4 %all-to-all-start.1 = ((bf16[8,4,8,512]{3,2,0,1:T(8,128)(2,1)}), bf16[8,4,8,512]{3,2,0,1:T(8,128)(2,1)S(1)}, u32[]{:S(2)}, u32[]{:S(2)}) async-start(bf16[8,4,8,512]{3,2,0,1:T(8,128)(2,1)} %copy.28), calls=%async_computation.1 | async-start | bytes 524288 | tf_op jit(solution)/shard_map/all_to_all | solution.py:61
  36.4 62.7 %all-gather.3.cloned.1.call-start = ((), (), s32[]{:S(2)}) async-start(), calls=%async_computation.3 | async-start | bytes 3899392 | tf_op jit(solution)/shard_map/all_gather | solution.py:75
  50.9 146.2 %reduce-scatter.4.cloned.1.call-start = ((), (), s32[]{:S(2)}) async-start(), calls=%async_computation.4 | async-start | bytes 3899392
  101.5 0.7 copy-start.2
  110.8 88.7 %copy-start.1 = (bf16[8,384,576]{1,2,0:T(8,128)(2,1)S(1)}, bf16[8,384,576]{1,2,0:T(8,128)(2,1)}, u32[]{:S(2)}) copy-start(bf16[8,384,576]{1,2,0:T(8,128)(2,1)} %param.15) | copy-start | bytes 10616836
Sparse Core Ops, SparseCore 0:
  51.0 48.0 all-gather.2
  129.6 67.3 reduce-scatter.3
